TPU v7x, 32 devices: a whole 2x2x4 slice. The times are simulated.
32 devices in a mesh: dp: 8 (over z, x), mp: 4 (over y, core).
Axes of the slice: x: 2, y: 2, z: 4, core: 2. Of those that a mesh axis runs over, the one named last changes fastest.
Arguments:
- teacher_states: bfloat16 [512, 128, 4096], P('dp', None, 'mp'), may hold values from -6 to 6
- teacher_gain: float32 [4096], P('mp'), may hold values from 0.25 to 1.75
- teacher_proj: bfloat16 [4096, 1024], P('mp'), may hold values from -0.09375 to 0.09375
- teacher_mask: int32 [512, 128], P('dp'), may hold values 0 or 1
- student_states: bfloat16 [1024, 64, 768], P(('dp', 'mp')), may hold values from -6 to 6
- student_gain: float32 [768], replicated, may hold values from 0.25 to 1.75
- student_proj: bfloat16 [768, 1024], replicated, may hold values from -0.21875 to 0.21875
- student_mask: int32 [1024, 64], P(('dp', 'mp')), may hold values 0 or 1
- positive: int32 [1024], P(('dp', 'mp')), may hold values from 0 to 511
Outputs:
- grad_embed: float32 [1024, 1024], P(('dp', 'mp'))
- grad_states: bfloat16 [1024, 64, 768], P(('dp', 'mp'))
All inputs are finite; a program needn't handle non-finite values. No bound on the sum of `teacher_mask` or of `student_mask` on one device may be relied on, other than what follows from the above.
Results may differ from a plain program's by a relative error of at most 0.0085.
Values may be sent and summed in bfloat16 or wider, within the bound.
A program may use at most 128 MiB of HBM per device.

v0:
```python
import jax
import jax.numpy as jnp
from jax import lax
from jax.sharding import PartitionSpec as P

D = 4096


def unit_rows(values):
    return (
        values
        * lax.rsqrt(jnp.mean(values * values, axis=-1, keepdims=True) + 1e-06)
        / jnp.sqrt(jnp.float32(values.shape[-1]))
    )


def student_forward(states, gain, proj, live_mask):
    values = states.astype(jnp.float32)
    scale = lax.rsqrt(jnp.mean(values * values, axis=-1, keepdims=True) + 1e-06)
    normed = (values * scale * gain).astype(jnp.bfloat16)
    flat = normed.reshape(-1, normed.shape[-1])
    act = jax.nn.gelu(jnp.dot(flat, proj, preferred_element_type=jnp.float32), approximate=True)
    act = act.reshape(states.shape[0], states.shape[1], -1)
    live = live_mask.astype(jnp.float32)
    pooled = jnp.sum(act * live[:, :, None], axis=1)
    return unit_rows(pooled)


def shards(
    teacher_states,
    teacher_gain,
    teacher_proj,
    teacher_mask,
    student_states,
    student_gain,
    student_proj,
    student_mask,
    positive,
):
    values = teacher_states.astype(jnp.float32)
    partial_squares = jnp.sum(values * values, axis=-1)
    squares = lax.psum(partial_squares, "mp")
    scale = lax.rsqrt(squares / D + 1e-06)
    live = teacher_mask.astype(jnp.float32)
    weight = live * scale
    pooled = jnp.sum(values * weight[:, :, None], axis=1)
    tpooled = (pooled * teacher_gain).astype(jnp.bfloat16)
    partial_embed = jnp.dot(tpooled, teacher_proj, preferred_element_type=jnp.float32)
    summed = lax.psum(partial_embed, "mp")
    group_emb = unit_rows(summed).astype(jnp.bfloat16)
    gathered = lax.all_gather(group_emb, "dp", axis=0, tiled=True)
    semb, back = jax.vjp(
        lambda st: student_forward(st, student_gain, student_proj, student_mask), student_states
    )
    sround = semb.astype(jnp.bfloat16)
    columns = lax.broadcasted_iota(jnp.int32, (positive.shape[0], gathered.shape[0]), 1)
    picker = (positive[:, None] == columns).astype(jnp.bfloat16)
    tpos = jnp.dot(picker, gathered, preferred_element_type=jnp.float32).astype(jnp.bfloat16)
    tlogit = 10.0 * jnp.dot(tpos, gathered.T, preferred_element_type=jnp.float32)
    slogit = 20.0 * jnp.dot(sround, gathered.T, preferred_element_type=jnp.float32)
    texp = jnp.exp(tlogit)
    sexp = jnp.exp(slogit)
    diff = (
        sexp / jnp.sum(sexp, axis=1, keepdims=True) - texp / jnp.sum(texp, axis=1, keepdims=True)
    ).astype(jnp.bfloat16)
    grad_embed = 20.0 * jnp.dot(diff, gathered, preferred_element_type=jnp.float32)
    grad_states = back(grad_embed)[0]
    return (grad_embed, grad_states)


def solution(mesh):
    in_specs = (
        P("dp", None, "mp"),
        P("mp"),
        P("mp", None),
        P("dp", None),
        P(("dp", "mp"), None, None),
        P(),
        P(),
        P(("dp", "mp"), None),
        P(("dp", "mp")),
    )
    out_specs = (P(("dp", "mp"), None), P(("dp", "mp"), None, None))
    return jax.shard_map(shards, mesh=mesh, in_specs=in_specs, out_specs=out_specs, check_vma=False)
```

profile of v0, /device:TPU:8, one launch (start us, length us, event | category | flops | bytes accessed | tf_op | source)
XLA Modules:
  0.0 153.5 jit_solution(10778247551571147130)
XLA Ops:
  7.2 0.0 all-reduce.2.cloned.1.call-start
  7.2 7.4 %fusion = f32[64,128]{1,0:T(8,128)S(1)} fusion(bf16[64,128,1024]{2,1,0:T(8,128)(2,1)} %param.9), kind=kLoop, calls=%fused_computation.2 | loop fusion | flops 25157632 | bytes 16809984 | tf_op jit(solution)/shard_map/reduce_sum | solution.py:41
  14.6 11.4 %psum.14 = f32[64,128]{1,0:T(8,128)S(1)} all-reduce(f32[64,128]{1,0:T(8,128)S(1)} %fusion), channel_id=1, replica_groups=mesh['dp'=8,'mp'=4] {'mp'}, use_global_device_ids=true, to_apply=%region_4.0 | all-reduce | flops 8192 | bytes 65536 | tf_op jit(solution)/shard_map/psum | solution.py:42
  26.2 7.6 %fusion.1 = f32[64,1024]{1,0:T(8,128)S(1)} fusion(bf16[64,128,1024]{2,1,0:T(8,128)(2,1)} %param.9, f32[64,128]{1,0:T(8,128)S(1)} %rsqrt_multiply_fusion), kind=kLoop, calls=%fused_computation.3 | loop fusion | flops 25100288 | bytes 17072128 | tf_op jit(solution)/shard_map/reduce_sum | solution.py:46
  33.8 1.2 fusion.31
  35.0 0.0 all-gather.2.cloned.1.call-start
  35.1 32.6 %all-reduce.2.cloned.1.call-done = f32[64,1024]{1,0:T(8,128)} async-done(((f32[64,1024]{1,0:T(8,128)}), f32[64,1024]{1,0:T(8,128)}) %all-reduce.2.cloned.1.call-update) | async-done | bytes 262160 | tf_op jit(solution)/shard_map/psum | solution.py:49
  67.7 1.1 multiply_reduce_fusion.1
  68.8 1.7 %multiply_convert_fusion = bf16[64,1024]{1,0:T(8,128)(2,1)} fusion(f32[64,1024]{1,0:T(8,128)} %all-reduce.2.cloned.1.call-done, f32[64]{0:T(128)S(1)} %add_rsqrt_fusion), kind=kLoop, calls=%fused_computation.43 | loop fusion | flops 196608 | bytes 393472 | tf_op jit(solution)/shard_map/convert_element_type | solution.py:50
  70.5 0.1 mul.250
  70.6 2.7 %fusion.17 = f32[32,64]{1,0:T(8,128)S(1)} fusion(bf16[32,64,768]{2,1,0:T(8,128)(2,1)} %param.13), kind=kLoop, calls=%fused_computation.28 | loop fusion | flops 4716544 | bytes 3153920 | tf_op jit(solution)/shard_map/jvp()/reduce_sum | solution.py:19
  73.3 2.7 %fusion.19 = bf16[32,64,768]{2,1,0:T(8,128)(2,1)S(1)} fusion(bf16[32,64,768]{2,1,0:T(8,128)(2,1)} %param.13, f32[768]{0:T(1024)S(1)} %copy-done.5, f32[32,64]{1,0:T(8,128)S(1)} %fusion.40), kind=kLoop, calls=%fused_computation.30 | loop fusion | flops 6291456 | bytes 6302720 | tf_op jit(solution)/shard_map/jvp()/convert_element_type | solution.py:20
  76.0 7.7 %multiply_reduce_fusion = (f32[32,1024]{1,0:T(8,128)S(1)}, f32[2048,1024]{1,0:T(8,128)}) fusion(f32[32,64]{1,0:T(8,128)S(1)} %convert_element_type.45, bf16[2048,768]{1,0:T(8,128)(2,1)S(1)} %bitcast.31, bf16[768,1024]{1,0:T(8,128)(2,1)S(1)} %copy-done.3), kind=kOutput, calls=%fused_computation.25 | convolution fusion | flops 3242164224 | bytes 13246464 | tf_op jit(solution)/shard_map/jvp()/dot_general | solution.py:22
  83.7 0.1 multiply_reduce_fusion.3
  83.8 26.0 %all-gather.2.cloned.1.call-done = bf16[512,1024]{1,0:T(8,128)(2,1)} async-done(((bf16[64,1024]{1,0:T(8,128)(2,1)}), bf16[512,1024]{1,0:T(8,128)(2,1)}) %all-gather.2.cloned.1.call-update) | async-done | bytes 1048592 | tf_op jit(solution)/shard_map/all_gather | solution.py:51
  109.8 2.5 %fusion.45 = (f32[32]{0:T(128)S(1)}, f32[32,512]{1,0:T(8,128)S(1)}) fusion(bf16[512,1024]{1,0:T(8,128)(2,1)} %all-gather.2.cloned.1.call-done, s32[32]{0:T(128)S(1)} %copy-done.9), kind=kOutput, calls=%fused_computation.73 | convolution fusion | flops 67190752 | bytes 1114368 | tf_op jit(solution)/shard_map/dot_general | solution.py:59
  112.2 1.8 %fusion.46 = (f32[32]{0:T(128)S(1)}, f32[32,512]{1,0:T(8,128)S(1)}) fusion(bf16[512,1024]{1,0:T(8,128)(2,1)} %all-gather.2.cloned.1.call-done, f32[32,1024]{1,0:T(8,128)S(1)} %get-tuple-element.8, f32[32]{0:T(128)S(1)} %fusion.41), kind=kOutput, calls=%fused_computation.74 | convolution fusion | flops 33685472 | bytes 1245440 | tf_op jit(solution)/shard_map/dot_general | solution.py:60
  114.0 1.7 %multiply_reduce_fusion.2 = (f32[32]{0:T(128)S(1)}, f32[32,1024]{1,0:T(8,128)S(1)}) fusion(f32[32,1024]{1,0:T(8,128)S(1)} %get-tuple-element.8, bf16[512,1024]{1,0:T(8,128)(2,1)} %all-gather.2.cloned.1.call-done, f32[32,512]{1,0:T(8,128)S(1)} %get-tuple-element.11, f32[32,512]{1,0:T(8,128)S(1)} %get-tuple-element.13, f32[32]{0:T(128)S(1)} %get-tuple-element.10, ...), kind=kOutput, calls=%fused_computation.48 | convolution fusion | flops 33718240 | bytes 1442176 | tf_op jit(solution)/shard_map/dot_general | solution.py:66
  115.7 0.7 add_add_fusion.1
  116.4 11.1 %fusion.14 = (f32[2048,1024]{1,0:T(8,128)}, f32[2048,1024]{1,0:T(8,128)}) fusion(f32[2048,1024]{1,0:T(8,128)} %get-tuple-element.9, f32[2048]{0:T(1024)S(1)} %mul.250, f32[32,1024]{1,0:T(8,128)S(1)} %get-tuple-element.4), kind=kLoop, calls=%fused_computation.23 | loop fusion | flops 33554432 | bytes 25305088 | tf_op jit(solution)/shard_map/transpose(jvp())/mul | solution.py:22
  127.5 11.6 %fusion.24 = bf16[2048,768]{1,0:T(8,128)(2,1)} fusion(bf16[768,1024]{1,0:T(8,128)(2,1)S(1)} %copy-done.4, f32[2048,1024]{1,0:T(8,128)} %get-tuple-element.3, f32[2048,1024]{1,0:T(8,128)S(1)} %bitcast.29, f32[2048,1024]{1,0:T(8,128)} %get-tuple-element.2), kind=kOutput, calls=%fused_computation.36 | convolution fusion | flops 3233284096 | bytes 29884416 | tf_op jit(solution)/shard_map/transpose(jvp())/dot_general | solution.py:22
  139.2 4.1 %fusion.20 = f32[32,64]{1,0:T(8,128)S(1)} fusion(bf16[32,64,768]{2,1,0:T(8,128)(2,1)} %param.13, bf16[32,64,768]{2,1,0:T(8,128)(2,1)} %bitcast.30, f32[768]{0:T(1024)S(1)} %copy-done.5), kind=kLoop, calls=%fused_computation.31 | loop fusion | flops 7862272 | bytes 6302720 | tf_op jit(solution)/shard_map/transpose(jvp())/reduce_sum | solution.py:20
  143.2 0.6 copy-done.2
  143.8 2.8 %fusion.16 = bf16[32,64,768]{2,1,0:T(8,128)(2,1)} fusion(bf16[32,64,768]{2,1,0:T(8,128)(2,1)S(1)} %copy-done.1, f32[32,64]{1,0:T(8,128)S(1)} %multiply_multiply_fusion.3, f32[768]{0:T(1024)S(1)} %copy-done.5, f32[32,64]{1,0:T(8,128)S(1)} %fusion.40, bf16[2048,768]{1,0:T(8,128)(2,1)S(1)} %copy-done.2), kind=kLoop, calls=%fused_computation.27 | loop fusion | flops 12582912 | bytes 9456640 | tf_op jit(solution)/shard_map/transpose(jvp())/convert_element_type | solution.py:18
  (33 shorter events, 0.2 us)
Async XLA Ops:
  7.2 26.6 %copy-start = (bf16[1024,1024]{1,0:T(8,128)(2,1)S(1)}, bf16[1024,1024]{1,0:T(8,128)(2,1)}, u32[]{:S(2)}) copy-start(bf16[1024,1024]{1,0:T(8,128)(2,1)} %param.11) | copy-start | bytes 6291460
  7.2 18.9 %copy-start.6 = (s32[64,128]{1,0:T(8,128)S(1)}, s32[64,128]{1,0:T(8,128)}, u32[]{:S(2)}) copy-start(s32[64,128]{1,0:T(8,128)} %param.12) | copy-start | bytes 98308
  7.2 60.5 %all-reduce.2.cloned.1.call-start = ((), (), s32[]{:S(2)}) async-start(), calls=%async_computation | async-start | bytes 524288 | tf_op jit(solution)/shard_map/psum | solution.py:49
  26.1 7.7 %copy-start.8 = (f32[1024]{0:T(1024)S(1)}, f32[1024]{0:T(1024)}, u32[]{:S(2)}) copy-start(f32[1024]{0:T(1024)} %param.10) | copy-start | bytes 12292
  26.1 44.4 %copy-start.7 = (s32[32,64]{1,0:T(8,128)S(1)}, s32[32,64]{1,0:T(8,128)}, u32[]{:S(2)}) copy-start(s32[32,64]{1,0:T(8,128)} %param.16) | copy-start | bytes 24580
  26.1 47.2 %copy-start.5 = (f32[768]{0:T(1024)S(1)}, f32[768]{0:T(1024)}, u32[]{:S(2)}) copy-start(f32[768]{0:T(1024)} %param.14) | copy-start | bytes 9220
  35.0 74.7 %all-gather.2.cloned.1.call-start = ((), (), s32[]{:S(2)}) async-start(), calls=%async_computation.1 | async-start | bytes 1179648 | tf_op jit(solution)/shard_map/all_gather | solution.py:51
  70.6 5.4 %copy-start.3 = (bf16[768,1024]{1,0:T(8,128)(2,1)S(1)}, bf16[768,1024]{1,0:T(8,128)(2,1)}, u32[]{:S(2)}) copy-start(bf16[768,1024]{1,0:T(8,128)(2,1)} %param.15) | copy-start | bytes 4718596
  73.3 36.5 %copy-start.9 = (s32[32]{0:T(128)S(1)}, s32[32]{0:T(128)}, u32[]{:S(2)}) copy-start(s32[32]{0:T(128)} %param.17) | copy-start | bytes 388
  115.7 11.8 %slice-start = ((s8[8388608]{0:T(1024)(128)(4,1)}), s8[4194304]{0:T(1024)(128)(4,1)S(1)}, s32[]{:S(2)}) async-start(s8[8388608]{0:T(1024)(128)(4,1)} %bitcast.28), calls=%async_computation.2 | async-start | bytes 8388608
  116.4 11.1 %slice-start.1 = ((s8[8388608]{0:T(1024)(128)(4,1)}), s8[4194304]{0:T(1024)(128)(4,1)S(1)}, s32[]{:S(2)}) async-start(s8[8388608]{0:T(1024)(128)(4,1)} %bitcast.28), calls=%async_computation.3 | async-start | bytes 8388608
  116.4 11.1 %copy-start.4 = (bf16[768,1024]{1,0:T(8,128)(2,1)S(1)}, bf16[768,1024]{1,0:T(8,128)(2,1)}, u32[]{:S(2)}) copy-start(bf16[768,1024]{1,0:T(8,128)(2,1)} %param.15) | copy-start | bytes 4718596
  139.1 4.1 %copy-start.1 = (bf16[32,64,768]{2,1,0:T(8,128)(2,1)S(1)}, bf16[32,64,768]{2,1,0:T(8,128)(2,1)}, u32[]{:S(2)}) copy-start(bf16[32,64,768]{2,1,0:T(8,128)(2,1)} %param.13) | copy-start | bytes 9437188
  139.2 4.7 %copy-start.2 = (bf16[2048,768]{1,0:T(8,128)(2,1)S(1)}, bf16[2048,768]{1,0:T(8,128)(2,1)}, u32[]{:S(2)}) copy-start(bf16[2048,768]{1,0:T(8,128)(2,1)} %fusion.24) | copy-start | bytes 9437188
Sparse Core Ops, SparseCore 0:
  35.2 32.4 all-reduce.1
  70.6 39.1 all-gather.1
where the time goes:
time: 157 us; the launch traced here: 153 us
  waiting for transfers between devices  58.6 us (37%)
  other arithmetic  41.9 us (27%)
  matrix products  26.4 us (17%)
  between operations  14.2 us (9%)
  blocking collectives  11.4 us (7%)
    psum x1, waiting for transfers between devices, shards(): summed = lax.psum(partial_embed, 'mp')  32.6 us
    all_gather x1, waiting for transfers between devices, shards(): gathered = lax.all_gather(group_emb, 'dp', axis=0, tiled=True)  26 us
    dot_general x2, matrix products, student_forward(): jnp.dot(flat, proj, preferred_element_type=jnp.float32)  19.3 us
    psum x1, blocking collectives, shards(): squares = lax.psum(partial_squares, 'mp')  11.4 us
    mul x1, other arithmetic, student_forward(): jax.nn.gelu(jnp.dot(flat, proj, preferred_element_type=jnp.float32), appr...  11.1 us
    reduce_sum x1, other arithmetic, shards(): pooled = jnp.sum(values * weight[:, :, None], axis=1)  7.65 us
    reduce_sum x1, other arithmetic, shards(): partial_squares = jnp.sum(values * values, axis=-1)  7.38 us
    reduce_sum x1, other arithmetic, student_forward(): normed = (values * scale * gain).astype(jnp.bfloat16)  4.07 us
  transfers between devices with their start and end apart: 2, of which 2 were waited for; matrix products, arithmetic and copies ran while one was open for 9% of the time, Pallas kernels for 0%

commit v1 on v0

v1 whole, which is shorter than its diff:
```python
import functools

import jax
import jax.numpy as jnp
from jax import lax
from jax.experimental import pallas as pl
from jax.experimental.pallas import tpu as pltpu
from jax.sharding import PartitionSpec as P

MESH = pl.DeviceIdType.MESH
F32 = jnp.float32
BF16 = jnp.bfloat16
GROUPS = 4
QC = 4
ROOT = 0.7978845608028654
CUBE = 0.044715
NT = (((1,), (1,)), ((), ()))


def spread(live, chunk, tokens):
    queries, length = live.shape
    wide = jnp.concatenate([live] * (tokens // length), axis=1)
    row = lax.broadcasted_iota(jnp.int32, (queries, tokens), 0)
    col = lax.broadcasted_iota(jnp.int32, (queries, tokens), 1)
    return jnp.where(row == chunk * (tokens // length) + col // length, wide, 0.0)


def front(
    dn, n, ts, tmask, tgain, tproj, ss, sgain, sproj, smask,
    temb_out, raw_out, h_out,
    tx, tp, sx, sp, sq, sqr, tpool, pf, pb, pr, te, hbuf,
    sem_tx, sem_in, sq_send, sq_recv, rs_send, rs_recv, ag_send, ag_recv, dp_send, dp_recv, h_sem, out_sem,
):
    passages, length, feats = tx.shape
    width = n * feats
    rows = passages // n
    embed = tp.shape[1]
    chunks = passages // 8
    tokens = QC * smask.shape[1]
    schunks = sx.shape[0] // tokens
    me_d, me_m = lax.axis_index("dp"), lax.axis_index("mp")

    def mp_peer(o):
        return (me_d, lax.rem(me_m + o, n))

    def dp_peer(o):
        return (lax.rem(me_d + o, dn), me_m)

    def load(c):
        part = pl.ds(c * 8, 8)
        return pltpu.make_async_copy(ts.at[part], tx.at[part], sem_tx.at[c])

    others = [
        pltpu.make_async_copy(ss, sx, sem_in.at[0]),
        pltpu.make_async_copy(sproj, sp, sem_in.at[1]),
        pltpu.make_async_copy(tproj, tp, sem_in.at[2]),
    ]
    for c in range(chunks):
        load(c).start()
    for copy in others:
        copy.start()
    barrier = pltpu.get_barrier_semaphore()
    for o in range(1, n):
        pl.semaphore_signal(barrier, inc=1, device_id=mp_peer(o), device_id_type=MESH)
    for o in range(1, dn):
        pl.semaphore_signal(barrier, inc=1, device_id=dp_peer(o), device_id_type=MESH)

    def remote(src, dst, send, recv, peer):
        return pltpu.make_async_remote_copy(
            src_ref=src, dst_ref=dst, send_sem=send, recv_sem=recv, device_id=peer, device_id_type=MESH
        )

    ones = jnp.ones((16, 128), BF16)
    row8 = lax.broadcasted_iota(jnp.int32, (8, length), 0)
    per = chunks // GROUPS
    sq_copies = []
    for g in range(GROUPS):

        def squares(i, carry):
            c = g * per + i
            load(c).wait()
            held = jnp.zeros((8, length), F32)
            for j in range(8):
                total = None
                for k in range(feats // 128):
                    x = tx[c * 8 + j, :, k * 128 : (k + 1) * 128].astype(F32)
                    total = x * x if total is None else total + x * x
                line = lax.dot_general(ones, total.astype(BF16), NT, preferred_element_type=F32)
                held = jnp.where(row8 == j, line[:8], held)
            sq[c] = held
            return carry

        lax.fori_loop(0, per, squares, 0)
        if g == 0:
            pl.semaphore_wait(barrier, n + dn - 2)
        part = pl.ds(g * per, per)
        for o in range(1, n):
            copy = remote(sq.at[part], sqr.at[o, part], sq_send.at[o, g], sq_recv.at[o, g], mp_peer(o))
            copy.start()
            sq_copies.append(copy)

    row16 = lax.rem(lax.broadcasted_iota(jnp.int32, (16, length), 0), 8)
    for g in range(GROUPS):
        for o in range(1, n):
            sq_copies[g * (n - 1) + o - 1].wait_recv()

        def pool(i, carry):
            c = g * per + i
            total = sq[c]
            for o in range(1, n):
                total = total + sqr[o, c]
            part = pl.ds(pl.multiple_of(c * 8, 8), 8)
            weight = tmask[part, :].astype(F32) * lax.rsqrt(total / width + 1e-06)
            high = weight.astype(BF16).astype(F32)
            both = jnp.concatenate([high, weight - high], axis=0)
            left = jnp.concatenate([jnp.where(row16 == j, both, 0.0) for j in range(8)], axis=1).astype(BF16)
            sums = jnp.dot(left, tx[pl.ds(c * 8, 8)].reshape(8 * length, feats), preferred_element_type=F32)
            tpool[part, :] = (sums[:8] + sums[8:]) * tgain[...]
            return carry

        lax.fori_loop(0, per, pool, 0)

    others[2].wait()
    partial = jnp.dot(tpool[...].astype(BF16), tp[...], preferred_element_type=F32)
    for j in range(n):
        block = partial[j * rows : (j + 1) * rows]
        pf[j] = block
        pb[j] = block.astype(BF16)
    rs_copies = []
    for o in range(1, n):
        copy = remote(pb.at[lax.rem(me_m + o, n)], pr.at[o], rs_send.at[o], rs_recv.at[o], mp_peer(o))
        copy.start()
        rs_copies.append(copy)

    live = smask[...].astype(F32)
    raw_out[...] = jnp.zeros_like(raw_out)
    others[0].wait()
    others[1].wait()

    def keep(i):
        part = pl.ds(pl.multiple_of(i * tokens, tokens), tokens)
        return pltpu.make_async_copy(hbuf.at[part], h_out.at[part], h_sem.at[i])

    def student(i, carry):
        part = pl.ds(pl.multiple_of(i * tokens, tokens), tokens)
        x = sx[part, :].astype(F32)
        scale = lax.rsqrt(jnp.mean(x * x, axis=-1, keepdims=True) + 1e-06)
        normed = (x * scale * sgain[...]).astype(BF16)
        picks = spread(live, i, tokens).astype(BF16)
        for k in range(embed // 256):
            cols = slice(k * 256, (k + 1) * 256)
            u = jnp.dot(normed, sp[:, cols], preferred_element_type=F32)
            uu = u * u
            th = jnp.tanh(u * (ROOT + (ROOT * CUBE) * uu))
            half = 0.5 + 0.5 * th
            act = u * half
            slope = half + act * (1.0 - th) * (ROOT + (3.0 * ROOT * CUBE) * uu)
            hbuf[part, cols] = slope.astype(BF16)
            raw_out[:, cols] += jnp.dot(picks, act.astype(BF16), preferred_element_type=F32)
        keep(i).start()
        return carry

    first, second = schunks // 4, schunks // 2
    lax.fori_loop(0, first, student, 0)

    for copy in rs_copies:
        copy.wait_recv()
    summed = pf[me_m]
    for o in range(1, n):
        summed = summed + pr[o].astype(F32)
    unit = summed * lax.rsqrt(jnp.mean(summed * summed, axis=-1, keepdims=True) + 1e-06) * (embed ** -0.5)
    te[me_d, me_m] = unit.astype(BF16)
    ag_copies = []
    for o in range(1, n):
        copy = remote(te.at[me_d, me_m], te.at[me_d, me_m], ag_send.at[o], ag_recv.at[o], mp_peer(o))
        copy.start()
        ag_copies.append(copy)

    lax.fori_loop(first, second, student, 0)

    for copy in ag_copies:
        copy.wait_recv()
    dp_copies = []
    for o in range(1, dn):
        copy = remote(te.at[me_d], te.at[me_d], dp_send.at[o], dp_recv.at[o], dp_peer(o))
        copy.start()
        dp_copies.append(copy)

    lax.fori_loop(second, schunks, student, 0)

    for copy in dp_copies:
        copy.wait_recv()
    out = pltpu.make_async_copy(te, temb_out, out_sem)
    out.start()
    for copy in sq_copies + rs_copies + ag_copies + dp_copies:
        copy.wait_send()
    for i in range(schunks):
        keep(i).wait()
    out.wait()


def back(temb, raw_ref, pos, smask, sgain, sproj, ss, h, embed_out, states_out, grad):
    step = pl.program_id(0)
    tokens = ss.shape[0]

    @pl.when(step == 0)
    def _():
        raw = raw_ref[...]
        width = raw.shape[1]
        scale = lax.rsqrt(jnp.mean(raw * raw, axis=-1, keepdims=True) + 1e-06)
        unit = scale * (width ** -0.5)
        sround = (raw * unit).astype(BF16)
        table = temb[...]
        columns = lax.broadcasted_iota(jnp.int32, (raw.shape[0], table.shape[0]), 1)
        picker = jnp.where(pos[...] == columns, 1.0, 0.0).astype(BF16)
        tpos = jnp.dot(picker, table, preferred_element_type=F32).astype(BF16)
        both = jnp.concatenate([tpos, sround], axis=0)
        logits = lax.dot_general(both, table, NT, preferred_element_type=F32)
        texp = jnp.exp(10.0 * logits[: raw.shape[0]])
        sexp = jnp.exp(20.0 * logits[raw.shape[0] :])
        diff = sexp / jnp.sum(sexp, axis=1, keepdims=True) - texp / jnp.sum(texp, axis=1, keepdims=True)
        ge = 20.0 * jnp.dot(diff.astype(BF16), table, preferred_element_type=F32)
        embed_out[...] = ge
        inner = jnp.mean(raw * ge, axis=-1, keepdims=True)
        grad[...] = unit * (ge - raw * (scale * scale * inner))

    picks = jnp.transpose(spread(smask[...].astype(F32), step, tokens)).astype(BF16)
    wide = jnp.dot(picks, grad[...].astype(BF16), preferred_element_type=F32)
    du = (h[...].astype(F32) * wide).astype(BF16)
    dn = lax.dot_general(du, sproj[...], NT, preferred_element_type=F32)
    gy = dn.astype(BF16).astype(F32) * sgain[...]
    x = ss[...].astype(F32)
    scale = lax.rsqrt(jnp.mean(x * x, axis=-1, keepdims=True) + 1e-06)
    inner = jnp.mean(x * gy, axis=-1, keepdims=True)
    states_out[...] = (scale * gy - x * (scale * scale * scale * inner)).astype(BF16)


def shards(dn, n, ts, tgain, tproj, tmask, ss, sgain, sproj, smask, positive):
    passages, length, feats = ts.shape
    embed = tproj.shape[1]
    queries, qlen, ds = ss.shape
    rows = passages // n
    total = queries * qlen
    tokens = QC * qlen
    schunks = total // tokens
    chunks = passages // 8
    flat = ss.reshape(total, ds)
    gain1 = sgain.reshape(1, ds)
    anyspace = pl.BlockSpec(memory_space=pl.ANY)
    vmem = pl.BlockSpec(memory_space=pltpu.VMEM)
    dma = pltpu.SemaphoreType.DMA
    temb, raw, h = pl.pallas_call(
        functools.partial(front, dn, n),
        out_shape=(
            jax.ShapeDtypeStruct((dn, n, rows, embed), BF16),
            jax.ShapeDtypeStruct((queries, embed), F32),
            jax.ShapeDtypeStruct((total, embed), BF16),
        ),
        in_specs=[anyspace, vmem, vmem, anyspace, anyspace, vmem, anyspace, vmem],
        out_specs=(anyspace, vmem, anyspace),
        scratch_shapes=[
            pltpu.VMEM((passages, length, feats), BF16),
            pltpu.VMEM((feats, embed), BF16),
            pltpu.VMEM((total, ds), BF16),
            pltpu.VMEM((ds, embed), BF16),
            pltpu.VMEM((chunks, 8, length), F32),
            pltpu.VMEM((n, chunks, 8, length), F32),
            pltpu.VMEM((passages, feats), F32),
            pltpu.VMEM((n, rows, embed), F32),
            pltpu.VMEM((n, rows, embed), BF16),
            pltpu.VMEM((n, rows, embed), BF16),
            pltpu.VMEM((dn, n, rows, embed), BF16),
            pltpu.VMEM((total, embed), BF16),
            dma((chunks,)),
            dma((3,)),
            dma((n, GROUPS)),
            dma((n, GROUPS)),
            dma((n,)),
            dma((n,)),
            dma((n,)),
            dma((n,)),
            dma((dn,)),
            dma((dn,)),
            dma((schunks,)),
            dma,
        ],
        compiler_params=pltpu.CompilerParams(
            collective_id=0, has_side_effects=True, vmem_limit_bytes=56 * 1024 * 1024
        ),
        name="front",
    )(ts, tmask, tgain.reshape(1, feats), tproj, flat, gain1, sproj, smask)
    fixed = lambda shape: pl.BlockSpec(shape, lambda i: (0,) * len(shape))
    grad_embed, grad_states = pl.pallas_call(
        back,
        grid=(schunks,),
        out_shape=(
            jax.ShapeDtypeStruct((queries, embed), F32),
            jax.ShapeDtypeStruct((total, ds), BF16),
        ),
        in_specs=[
            fixed((dn * passages, embed)),
            fixed((queries, embed)),
            fixed((queries, 1)),
            fixed((queries, qlen)),
            fixed((1, ds)),
            fixed((ds, embed)),
            pl.BlockSpec((tokens, ds), lambda i: (i, 0)),
            pl.BlockSpec((tokens, embed), lambda i: (i, 0)),
        ],
        out_specs=(fixed((queries, embed)), pl.BlockSpec((tokens, ds), lambda i: (i, 0))),
        scratch_shapes=[pltpu.VMEM((queries, embed), F32)],
        compiler_params=pltpu.CompilerParams(vmem_limit_bytes=40 * 1024 * 1024),
        name="back",
    )(temb.reshape(dn * passages, embed), raw, positive.reshape(queries, 1), smask, gain1, sproj, flat, h)
    return grad_embed, grad_states.reshape(queries, qlen, ds)


def solution(mesh):
    in_specs = (
        P("dp", None, "mp"),
        P("mp"),
        P("mp", None),
        P("dp", None),
        P(("dp", "mp"), None, None),
        P(),
        P(),
        P(("dp", "mp"), None),
        P(("dp", "mp")),
    )
    out_specs = (P(("dp", "mp"), None), P(("dp", "mp"), None, None))
    body = functools.partial(shards, mesh.shape["dp"], mesh.shape["mp"])
    return jax.shard_map(body, mesh=mesh, in_specs=in_specs, out_specs=out_specs, check_vma=False)
```

time: 157 us -> 66.4 us (0.42)
  the two profiles are of different devices: /device:TPU:8 before, /device:TPU:10 now
where the time goes in v1:
time: 66.4 us; the launch traced here: 66.1 us
  Pallas kernels  59.1 us (89%)
  local copies, waits for them, and re-layouts  6.33 us (10%)
  between operations  0.69 us (1%)
    pallas_call x1, Pallas kernels, shards(): pl.pallas_call(functools.partial(front, dn, n), out_shape=(jax.ShapeDtype...  48.7 us
    pallas_call x1, Pallas kernels, shards(): pl.pallas_call(back, grid=(schunks,), out_shape=(jax.ShapeDtypeStruct((qu...  10.4 us
    unnamed x14, local copies, waits for them, and re-layouts  4.33 us

profile of v1, /device:TPU:10, one launch (start us, length us, event | category | flops | bytes accessed | tf_op | source)
XLA Modules:
  0.0 66.1 jit_solution(10259269732160478063)
XLA Ops:
  0.6 1.3 %reshape.24.sgain = f32[1,768]{1,0:T(1,128)} reshape(f32[768]{0:T(1024)} %param.14) | data formatting | bytes 6144 | tf_op jit(solution)/shard_map/reshape | solution.py:248
  1.9 0.7 %copy.11.pos = s32[32,1]{1,0:T(8,128)S(1)} copy(s32[32,1]{0,1:T(1,128)} %bitcast.9) | data formatting | bytes 256 | tf_op jit(solution)/shard_map/reshape | solution.py:314
  2.6 0.0 copy-start
  2.6 0.0 copy-start.1
  2.6 0.0 copy-start.5
  2.6 0.0 copy-start.6
  2.7 48.7 %front.1 = (bf16[8,4,16,1024]{3,2,1,0:T(8,128)(2,1)}, f32[32,1024]{1,0:T(8,128)}, bf16[2048,1024]{1,0:T(8,128)(2,1)}) custom-call(bf16[64,128,1024]{2,1,0:T(8,128)(2,1)} %ts.1, s32[64,128]{1,0:T(8,128)} %tmask.1, f32[1,1024]{1,0:T(1,128)} %bitcast.8, bf16[1024,1024]{1,0:T(8,128)(2,1)} %tproj.1, bf16[2048,768]{1,0:T(8,128)(2,1)} %bitcast.5, ...), custom_call_target="tpu_custom_call" | custom-call | tf_op jit(solution)/shard_map/front/pallas_call | solution.py:252
  51.3 0.0 copy-done
  51.4 0.0 copy-done.1
  51.4 0.0 copy-done.5
  51.4 0.0 copy-done.6
  51.4 0.0 copy-start.2
  51.4 2.2 %copy-done.2 = bf16[2048,1024]{1,0:T(8,128)(2,1)S(1)} copy-done((bf16[2048,1024]{1,0:T(8,128)(2,1)S(1)}, bf16[2048,1024]{1,0:T(8,128)(2,1)}, u32[]{:S(2)}) %copy-start.2) | copy-done | bytes 4194328
  53.6 0.0 copy-start.3
  53.6 1.2 %copy-done.3 = bf16[8,4,16,1024]{3,2,1,0:T(8,128)(2,1)S(1)} copy-done((bf16[8,4,16,1024]{3,2,1,0:T(8,128)(2,1)S(1)}, bf16[8,4,16,1024]{3,2,1,0:T(8,128)(2,1)}, u32[]{:S(2)}) %copy-start.3) | copy-done | bytes 1048600
  54.8 0.0 copy-start.4
  54.8 0.9 %copy-done.4 = f32[32,1024]{1,0:T(8,128)S(1)} copy-done((f32[32,1024]{1,0:T(8,128)S(1)}, f32[32,1024]{1,0:T(8,128)}, u32[]{:S(2)}) %copy-start.4) | copy-done | bytes 131096
  55.7 10.4 %back.1 = (f32[32,1024]{1,0:T(8,128)}, bf16[2048,768]{1,0:T(8,128)(2,1)}) custom-call(bf16[512,1024]{1,0:T(8,128)(2,1)S(1)} %bitcast.7, f32[32,1024]{1,0:T(8,128)S(1)} %copy-done.4, s32[32,1]{1,0:T(8,128)S(1)} %copy.11.pos, s32[32,64]{1,0:T(8,128)S(1)} %copy-done.5, f32[1,768]{1,0:T(1,128)S(1)} %copy-done.6, bf16[768,1024]{1,0:T(8,128)(2,1)S(1)} %copy-done.1, ...), custom_call_target="tpu_custom_call" | custom-call | tf_op jit(solution)/shard_map/back/pallas_call | solution.py:293
Async XLA Ops:
  2.6 48.7 %copy-start = (bf16[32,64,768]{2,1,0:T(8,128)(2,1)S(1)}, bf16[32,64,768]{2,1,0:T(8,128)(2,1)}, u32[]{:S(2)}) copy-start(bf16[32,64,768]{2,1,0:T(8,128)(2,1)} %param.13) | copy-start | bytes 9437188
  2.6 48.7 %copy-start.1 = (bf16[768,1024]{1,0:T(8,128)(2,1)S(1)}, bf16[768,1024]{1,0:T(8,128)(2,1)}, u32[]{:S(2)}) copy-start(bf16[768,1024]{1,0:T(8,128)(2,1)} %sproj.3) | copy-start | bytes 4718596
  2.6 48.7 %copy-start.5 = (s32[32,64]{1,0:T(8,128)S(1)}, s32[32,64]{1,0:T(8,128)}, u32[]{:S(2)}) copy-start(s32[32,64]{1,0:T(8,128)} %smask.3) | copy-start | bytes 24580
  2.6 48.7 %copy-start.6 = (f32[1,768]{1,0:T(1,128)S(1)}, f32[1,768]{1,0:T(1,128)}, u32[]{:S(2)}) copy-start(f32[1,768]{1,0:T(1,128)} %reshape.24.sgain) | copy-start | bytes 9220
  51.4 2.2 %copy-start.2 = (bf16[2048,1024]{1,0:T(8,128)(2,1)S(1)}, bf16[2048,1024]{1,0:T(8,128)(2,1)}, u32[]{:S(2)}) copy-start(bf16[2048,1024]{1,0:T(8,128)(2,1)} %get-tuple-element.9.h) | copy-start | bytes 12582916
  53.6 1.2 %copy-start.3 = (bf16[8,4,16,1024]{3,2,1,0:T(8,128)(2,1)S(1)}, bf16[8,4,16,1024]{3,2,1,0:T(8,128)(2,1)}, u32[]{:S(2)}) copy-start(bf16[8,4,16,1024]{3,2,1,0:T(8,128)(2,1)} %get-tuple-element.7) | copy-start | bytes 3145732
  54.8 0.9 %copy-start.4 = (f32[32,1024]{1,0:T(8,128)S(1)}, f32[32,1024]{1,0:T(8,128)}, u32[]{:S(2)}) copy-start(f32[32,1024]{1,0:T(8,128)} %get-tuple-element.8.raw_ref) | copy-start | bytes 393220

commit v2 on v1

--- a/solution.py
+++ b/solution.py
@@ -26,10 +26,10 @@
 
 
 def front(
-    dn, n, ts, tmask, tgain, tproj, ss, sgain, sproj, smask,
-    temb_out, raw_out, h_out,
-    tx, tp, sx, sp, sq, sqr, tpool, pf, pb, pr, te, hbuf,
-    sem_tx, sem_in, sq_send, sq_recv, rs_send, rs_recv, ag_send, ag_recv, dp_send, dp_recv, h_sem, out_sem,
+    dn, n, ts, tmask, tgain, tproj, ss, sgain, sproj, smask, pos,
+    embed_out, grad_out, h_out,
+    tx, tp, sx, sp, sq, sqr, tpool, pf, pb, pr, te, hbuf, raw_out,
+    sem_tx, sem_in, sq_send, sq_recv, rs_send, rs_recv, ag_send, ag_recv, dp_send, dp_recv, fw_send, fw_recv, h_sem,
 ):
     passages, length, feats = tx.shape
     width = n * feats
@@ -115,7 +115,7 @@
             both = jnp.concatenate([high, weight - high], axis=0)
             left = jnp.concatenate([jnp.where(row16 == j, both, 0.0) for j in range(8)], axis=1).astype(BF16)
             sums = jnp.dot(left, tx[pl.ds(c * 8, 8)].reshape(8 * length, feats), preferred_element_type=F32)
-            tpool[part, :] = (sums[:8] + sums[8:]) * tgain[...]
+            tpool[part, :] = (sums[:8] + sums[8:]) * tgain[...].reshape(1, feats)
             return carry
 
         lax.fori_loop(0, per, pool, 0)
@@ -145,7 +145,7 @@
         part = pl.ds(pl.multiple_of(i * tokens, tokens), tokens)
         x = sx[part, :].astype(F32)
         scale = lax.rsqrt(jnp.mean(x * x, axis=-1, keepdims=True) + 1e-06)
-        normed = (x * scale * sgain[...]).astype(BF16)
+        normed = (x * scale * sgain[...].reshape(1, sx.shape[1])).astype(BF16)
         picks = spread(live, i, tokens).astype(BF16)
         for k in range(embed // 256):
             cols = slice(k * 256, (k + 1) * 256)
@@ -160,7 +160,7 @@
         keep(i).start()
         return carry
 
-    first, second = schunks // 4, schunks // 2
+    first, second, third = schunks // 4, 3 * schunks // 8, 7 * schunks // 8
     lax.fori_loop(0, first, student, 0)
 
     for copy in rs_copies:
@@ -181,54 +181,63 @@
     for copy in ag_copies:
         copy.wait_recv()
     dp_copies = []
+    half = n // 2
+    core = lax.rem(me_m, 2)
+    mine = pl.ds(core * half, half)
+    partner = (me_d, me_m + 1 - 2 * core)
     for o in range(1, dn):
-        copy = remote(te.at[me_d], te.at[me_d], dp_send.at[o], dp_recv.at[o], dp_peer(o))
+        copy = remote(te.at[me_d, mine], te.at[me_d, mine], dp_send.at[o], dp_recv.at[o], dp_peer(o))
         copy.start()
         dp_copies.append(copy)
 
-    lax.fori_loop(second, schunks, student, 0)
-
-    for copy in dp_copies:
+    lax.fori_loop(second, third, student, 0)
+
+    fw_copies = []
+    for o in range(1, dn):
+        dp_copies[o - 1].wait_recv()
+        came = te.at[lax.rem(me_d + dn - o, dn), mine]
+        copy = remote(came, came, fw_send.at[o], fw_recv.at[o], partner)
+        copy.start()
+        fw_copies.append(copy)
+
+    lax.fori_loop(third, schunks, student, 0)
+
+    raw = raw_out[...]
+    queries = raw.shape[0]
+    scale = lax.rsqrt(jnp.mean(raw * raw, axis=-1, keepdims=True) + 1e-06)
+    unit = scale * (embed ** -0.5)
+    sround = (raw * unit).astype(BF16)
+    total = dn * passages
+    lines = lax.broadcasted_iota(jnp.int32, (total, queries), 0)
+    picker = jnp.transpose(jnp.where(pos[...].reshape(1, queries) == lines, 1.0, 0.0)).astype(BF16)
+
+    for copy in fw_copies:
         copy.wait_recv()
-    out = pltpu.make_async_copy(te, temb_out, out_sem)
-    out.start()
-    for copy in sq_copies + rs_copies + ag_copies + dp_copies:
+    table = te[...].reshape(total, embed)
+    tpos = jnp.dot(picker, table, preferred_element_type=F32).astype(BF16)
+    both = jnp.concatenate([tpos, sround], axis=0)
+    logits = lax.dot_general(both, table, NT, preferred_element_type=F32)
+    texp = jnp.exp(10.0 * logits[:queries])
+    sexp = jnp.exp(20.0 * logits[queries:])
+    diff = sexp / jnp.sum(sexp, axis=1, keepdims=True) - texp / jnp.sum(texp, axis=1, keepdims=True)
+    ge = 20.0 * jnp.dot(diff.astype(BF16), table, preferred_element_type=F32)
+    embed_out[...] = ge
+    inner = jnp.mean(raw * ge, axis=-1, keepdims=True)
+    grad_out[...] = unit * (ge - raw * (scale * scale * inner))
+    for copy in sq_copies + rs_copies + ag_copies + dp_copies + fw_copies:
         copy.wait_send()
     for i in range(schunks):
         keep(i).wait()
-    out.wait()
-
-
-def back(temb, raw_ref, pos, smask, sgain, sproj, ss, h, embed_out, states_out, grad):
+
+
+def back(grad, smask, sgain, sproj, ss, h, states_out):
     step = pl.program_id(0)
     tokens = ss.shape[0]
-
-    @pl.when(step == 0)
-    def _():
-        raw = raw_ref[...]
-        width = raw.shape[1]
-        scale = lax.rsqrt(jnp.mean(raw * raw, axis=-1, keepdims=True) + 1e-06)
-        unit = scale * (width ** -0.5)
-        sround = (raw * unit).astype(BF16)
-        table = temb[...]
-        columns = lax.broadcasted_iota(jnp.int32, (raw.shape[0], table.shape[0]), 1)
-        picker = jnp.where(pos[...] == columns, 1.0, 0.0).astype(BF16)
-        tpos = jnp.dot(picker, table, preferred_element_type=F32).astype(BF16)
-        both = jnp.concatenate([tpos, sround], axis=0)
-        logits = lax.dot_general(both, table, NT, preferred_element_type=F32)
-        texp = jnp.exp(10.0 * logits[: raw.shape[0]])
-        sexp = jnp.exp(20.0 * logits[raw.shape[0] :])
-        diff = sexp / jnp.sum(sexp, axis=1, keepdims=True) - texp / jnp.sum(texp, axis=1, keepdims=True)
-        ge = 20.0 * jnp.dot(diff.astype(BF16), table, preferred_element_type=F32)
-        embed_out[...] = ge
-        inner = jnp.mean(raw * ge, axis=-1, keepdims=True)
-        grad[...] = unit * (ge - raw * (scale * scale * inner))
-
     picks = jnp.transpose(spread(smask[...].astype(F32), step, tokens)).astype(BF16)
     wide = jnp.dot(picks, grad[...].astype(BF16), preferred_element_type=F32)
     du = (h[...].astype(F32) * wide).astype(BF16)
     dn = lax.dot_general(du, sproj[...], NT, preferred_element_type=F32)
-    gy = dn.astype(BF16).astype(F32) * sgain[...]
+    gy = dn.astype(BF16).astype(F32) * sgain[...].reshape(1, ss.shape[1])
     x = ss[...].astype(F32)
     scale = lax.rsqrt(jnp.mean(x * x, axis=-1, keepdims=True) + 1e-06)
     inner = jnp.mean(x * gy, axis=-1, keepdims=True)
@@ -245,19 +254,18 @@
     schunks = total // tokens
     chunks = passages // 8
     flat = ss.reshape(total, ds)
-    gain1 = sgain.reshape(1, ds)
     anyspace = pl.BlockSpec(memory_space=pl.ANY)
     vmem = pl.BlockSpec(memory_space=pltpu.VMEM)
     dma = pltpu.SemaphoreType.DMA
-    temb, raw, h = pl.pallas_call(
+    grad_embed, grad, h = pl.pallas_call(
         functools.partial(front, dn, n),
         out_shape=(
-            jax.ShapeDtypeStruct((dn, n, rows, embed), BF16),
+            jax.ShapeDtypeStruct((queries, embed), F32),
             jax.ShapeDtypeStruct((queries, embed), F32),
             jax.ShapeDtypeStruct((total, embed), BF16),
         ),
-        in_specs=[anyspace, vmem, vmem, anyspace, anyspace, vmem, anyspace, vmem],
-        out_specs=(anyspace, vmem, anyspace),
+        in_specs=[anyspace, vmem, vmem, anyspace, anyspace, vmem, anyspace, vmem, vmem],
+        out_specs=(vmem, vmem, anyspace),
         scratch_shapes=[
             pltpu.VMEM((passages, length, feats), BF16),
             pltpu.VMEM((feats, embed), BF16),
@@ -271,6 +279,7 @@
             pltpu.VMEM((n, rows, embed), BF16),
             pltpu.VMEM((dn, n, rows, embed), BF16),
             pltpu.VMEM((total, embed), BF16),
+            pltpu.VMEM((queries, embed), F32),
             dma((chunks,)),
             dma((3,)),
             dma((n, GROUPS)),
@@ -281,37 +290,32 @@
             dma((n,)),
             dma((dn,)),
             dma((dn,)),
+            dma((dn,)),
+            dma((dn,)),
             dma((schunks,)),
-            dma,
         ],
         compiler_params=pltpu.CompilerParams(
             collective_id=0, has_side_effects=True, vmem_limit_bytes=56 * 1024 * 1024
         ),
         name="front",
-    )(ts, tmask, tgain.reshape(1, feats), tproj, flat, gain1, sproj, smask)
+    )(ts, tmask, tgain, tproj, flat, sgain, sproj, smask, positive)
     fixed = lambda shape: pl.BlockSpec(shape, lambda i: (0,) * len(shape))
-    grad_embed, grad_states = pl.pallas_call(
+    grad_states = pl.pallas_call(
         back,
         grid=(schunks,),
-        out_shape=(
-            jax.ShapeDtypeStruct((queries, embed), F32),
-            jax.ShapeDtypeStruct((total, ds), BF16),
-        ),
+        out_shape=jax.ShapeDtypeStruct((total, ds), BF16),
         in_specs=[
-            fixed((dn * passages, embed)),
             fixed((queries, embed)),
-            fixed((queries, 1)),
             fixed((queries, qlen)),
-            fixed((1, ds)),
+            fixed((ds,)),
             fixed((ds, embed)),
             pl.BlockSpec((tokens, ds), lambda i: (i, 0)),
             pl.BlockSpec((tokens, embed), lambda i: (i, 0)),
         ],
-        out_specs=(fixed((queries, embed)), pl.BlockSpec((tokens, ds), lambda i: (i, 0))),
-        scratch_shapes=[pltpu.VMEM((queries, embed), F32)],
-        compiler_params=pltpu.CompilerParams(vmem_limit_bytes=40 * 1024 * 1024),
+        out_specs=pl.BlockSpec((tokens, ds), lambda i: (i, 0)),
+        compiler_params=pltpu.CompilerParams(vmem_limit_bytes=62 * 1024 * 1024),
         name="back",
-    )(temb.reshape(dn * passages, embed), raw, positive.reshape(queries, 1), smask, gain1, sproj, flat, h)
+    )(grad, smask, sgain, sproj, flat, h)
     return grad_embed, grad_states.reshape(queries, qlen, ds)
 
 

time: 66.4 us -> 51.7 us (0.78)
  the two profiles are of different devices: /device:TPU:10 before, /device:TPU:8 now
where the time goes in v2:
time: 51.7 us; the launch traced here: 51.3 us
  Pallas kernels  50 us (97%)
  local copies, waits for them, and re-layouts  0.66 us (1%)
  between operations  0.65 us (1%)
    pallas_call x1, Pallas kernels, shards(): pl.pallas_call(functools.partial(front, dn, n), out_shape=(jax.ShapeDtype...  38.1 us
    pallas_call x1, Pallas kernels, shards(): pl.pallas_call(back, grid=(schunks,), out_shape=jax.ShapeDtypeStruct((tot...  11.9 us

profile of v2, /device:TPU:8, one launch (start us, length us, event | category | flops | bytes accessed | tf_op | source)
XLA Modules:
  0.0 51.3 jit_solution(6664420188591905953)
XLA Ops:
  0.6 38.1 %front.1 = (f32[32,1024]{1,0:T(8,128)}, f32[32,1024]{1,0:T(8,128)}, bf16[2048,1024]{1,0:T(8,128)(2,1)}) custom-call(bf16[64,128,1024]{2,1,0:T(8,128)(2,1)} %ts.1, s32[64,128]{1,0:T(8,128)} %tmask.1, f32[1024]{0:T(1024)} %tgain.1, bf16[1024,1024]{1,0:T(8,128)(2,1)} %tproj.1, bf16[2048,768]{1,0:T(8,128)(2,1)} %bitcast.2, f32[768]{0:T(1024)} %sgain.3, ...), custom_call_target="tpu_custom_call" | custom-call | tf_op jit(solution)/shard_map/front/pallas_call | solution.py:260
  38.7 0.0 copy-start
  38.7 11.9 %back.1 = bf16[2048,768]{1,0:T(8,128)(2,1)} custom-call(f32[32,1024]{1,0:T(8,128)} %get-tuple-element.6.grad, s32[32,64]{1,0:T(8,128)} %smask.3, f32[768]{0:T(1024)} %sgain.3, bf16[768,1024]{1,0:T(8,128)(2,1)} %sproj.3, bf16[2048,768]{1,0:T(8,128)(2,1)} %bitcast.3, bf16[2048,1024]{1,0:T(8,128)(2,1)} %get-tuple-element.7.h), custom_call_target="tpu_custom_call" | custom-call | tf_op jit(solution)/shard_map/back/pallas_call | solution.py:303
  50.7 0.0 copy-done
  50.7 0.7 %copy.12 = f32[32,1024]{1,0:T(8,128)} copy(f32[32,1024]{1,0:T(8,128)S(1)} %copy-done) | data formatting | bytes 262144
Async XLA Ops:
  38.7 11.9 %copy-start = (f32[32,1024]{1,0:T(8,128)S(1)}, f32[32,1024]{1,0:T(8,128)}, u32[]{:S(2)}) copy-start(f32[32,1024]{1,0:T(8,128)} %get-tuple-element.10) | copy-start | bytes 393220

commit v3 on v2

--- a/solution.py
+++ b/solution.py
@@ -55,10 +55,9 @@
         pltpu.make_async_copy(sproj, sp, sem_in.at[1]),
         pltpu.make_async_copy(tproj, tp, sem_in.at[2]),
     ]
-    for c in range(chunks):
+    ahead = min(4, chunks)
+    for c in range(ahead):
         load(c).start()
-    for copy in others:
-        copy.start()
     barrier = pltpu.get_barrier_semaphore()
     for o in range(1, n):
         pl.semaphore_signal(barrier, inc=1, device_id=mp_peer(o), device_id_type=MESH)
@@ -79,6 +78,11 @@
         def squares(i, carry):
             c = g * per + i
             load(c).wait()
+
+            @pl.when(c + ahead < chunks)
+            def _():
+                load(c + ahead).start()
+
             held = jnp.zeros((8, length), F32)
             for j in range(8):
                 total = None
@@ -93,6 +97,9 @@
         lax.fori_loop(0, per, squares, 0)
         if g == 0:
             pl.semaphore_wait(barrier, n + dn - 2)
+        if g == GROUPS // 2:
+            for copy in others:
+                copy.start()
         part = pl.ds(g * per, per)
         for o in range(1, n):
             copy = remote(sq.at[part], sqr.at[o, part], sq_send.at[o, g], sq_recv.at[o, g], mp_peer(o))
@@ -230,9 +237,14 @@
         keep(i).wait()
 
 
-def back(grad, smask, sgain, sproj, ss, h, states_out):
+def back(ge, grad, smask, sgain, sproj, ss, h, embed_out, states_out):
     step = pl.program_id(0)
     tokens = ss.shape[0]
+
+    @pl.when(step == 0)
+    def _():
+        embed_out[...] = ge[...]
+
     picks = jnp.transpose(spread(smask[...].astype(F32), step, tokens)).astype(BF16)
     wide = jnp.dot(picks, grad[...].astype(BF16), preferred_element_type=F32)
     du = (h[...].astype(F32) * wide).astype(BF16)
@@ -257,7 +269,7 @@
     anyspace = pl.BlockSpec(memory_space=pl.ANY)
     vmem = pl.BlockSpec(memory_space=pltpu.VMEM)
     dma = pltpu.SemaphoreType.DMA
-    grad_embed, grad, h = pl.pallas_call(
+    ge, grad, h = pl.pallas_call(
         functools.partial(front, dn, n),
         out_shape=(
             jax.ShapeDtypeStruct((queries, embed), F32),
@@ -300,11 +312,12 @@
         name="front",
     )(ts, tmask, tgain, tproj, flat, sgain, sproj, smask, positive)
     fixed = lambda shape: pl.BlockSpec(shape, lambda i: (0,) * len(shape))
-    grad_states = pl.pallas_call(
+    grad_embed, grad_states = pl.pallas_call(
         back,
         grid=(schunks,),
-        out_shape=jax.ShapeDtypeStruct((total, ds), BF16),
+        out_shape=(jax.ShapeDtypeStruct((queries, embed), F32), jax.ShapeDtypeStruct((total, ds), BF16)),
         in_specs=[
+            fixed((queries, embed)),
             fixed((queries, embed)),
             fixed((queries, qlen)),
             fixed((ds,)),
@@ -312,10 +325,10 @@
             pl.BlockSpec((tokens, ds), lambda i: (i, 0)),
             pl.BlockSpec((tokens, embed), lambda i: (i, 0)),
         ],
-        out_specs=pl.BlockSpec((tokens, ds), lambda i: (i, 0)),
+        out_specs=(fixed((queries, embed)), pl.BlockSpec((tokens, ds), lambda i: (i, 0))),
         compiler_params=pltpu.CompilerParams(vmem_limit_bytes=62 * 1024 * 1024),
         name="back",
-    )(grad, smask, sgain, sproj, flat, h)
+    )(ge, grad, smask, sgain, sproj, flat, h)
     return grad_embed, grad_states.reshape(queries, qlen, ds)
 
 

time: 51.7 us -> 49.9 us (0.965)
  Pallas kernels: 50 us -> 48.9 us
  local copies, waits for them, and re-layouts: 0.66 us -> 0 us
    pallas_call x1, Pallas kernels: 38.1 us -> 36.9 us  [shards(): pl.pallas_call(functools.partial(front, dn, n), out_shape=(jax.ShapeDtype...]
    unnamed x3 -> x0, local copies, waits for them, and re-layouts: 0.66 us -> none
where the time goes in v3:
time: 49.9 us; the launch traced here: 49.5 us
  Pallas kernels  48.9 us (98%)
  between operations  0.64 us (1%)
    pallas_call x1, Pallas kernels, shards(): pl.pallas_call(functools.partial(front, dn, n), out_shape=(jax.ShapeDtype...  36.9 us
    pallas_call x1, Pallas kernels, shards(): pl.pallas_call(back, grid=(schunks,), out_shape=(jax.ShapeDtypeStruct((qu...  12 us

profile of v3, /device:TPU:8, one launch (start us, length us, event | category | flops | bytes accessed | tf_op | source)
XLA Modules:
  0.0 49.5 jit_solution(1773787105313959876)
XLA Ops:
  0.6 36.9 %front.1 = (f32[32,1024]{1,0:T(8,128)}, f32[32,1024]{1,0:T(8,128)}, bf16[2048,1024]{1,0:T(8,128)(2,1)}) custom-call(bf16[64,128,1024]{2,1,0:T(8,128)(2,1)} %ts.1, s32[64,128]{1,0:T(8,128)} %tmask.1, f32[1024]{0:T(1024)} %tgain.1, bf16[1024,1024]{1,0:T(8,128)(2,1)} %tproj.1, bf16[2048,768]{1,0:T(8,128)(2,1)} %bitcast.2, f32[768]{0:T(1024)} %sgain.3, ...), custom_call_target="tpu_custom_call" | custom-call | tf_op jit(solution)/shard_map/front/pallas_call | solution.py:272
  37.6 12.0 %back.1 = (f32[32,1024]{1,0:T(8,128)}, bf16[2048,768]{1,0:T(8,128)(2,1)}) custom-call(f32[32,1024]{1,0:T(8,128)} %get-tuple-element.7.ge, f32[32,1024]{1,0:T(8,128)} %get-tuple-element.8.grad, s32[32,64]{1,0:T(8,128)} %smask.3, f32[768]{0:T(1024)} %sgain.3, bf16[768,1024]{1,0:T(8,128)(2,1)} %sproj.3, bf16[2048,768]{1,0:T(8,128)(2,1)} %bitcast.3, ...), custom_call_target="tpu_custom_call" | custom-call | tf_op jit(solution)/shard_map/back/pallas_call | solution.py:315
